TPU v7x, 32 devices: a whole 2x2x4 slice. The times are simulated.
32 devices in a mesh: mode: 8 (over z, y), cores: 4 (over x, core).
Axes of the slice: x: 2, y: 2, z: 4, core: 2. Of those that a mesh axis runs over, the one named last changes fastest.
Arguments:
- train_cores: bfloat16 [4, 400, 32, 400], P('cores', None, 'mode'), may hold values from -0.24748737 to 0.24748737
- sketch_cores: bfloat16 [4, 100, 32, 100], P('cores', None, 'mode'), may hold values from -0.3125 to 0.3125
- left_interface: float32 [100, 400], replicated, may hold values from -6 to 6
- right_sketch: bfloat16 [400, 100], replicated, may hold values from -6 to 6
Outputs:
- frames: bfloat16 [4, 100, 32, 100], P('cores', None, 'mode')
- interfaces: float32 [4, 100, 400], P('cores')
All inputs are finite; a program needn't handle non-finite values.
Results may differ from a plain program's by a relative error of at most 0.019.
Values may be sent and summed in bfloat16 or wider, within the bound.
A program may use at most 64 MiB of HBM per device.

v0:
```python
import math
import jax
import jax.numpy as jnp
from jax import lax
from jax.sharding import PartitionSpec as P


def from_behind(shard, axis, by):
    size = lax.axis_size(axis)
    pairs = [(i, i + by) for i in range(size) if 0 <= i + by < size]
    return lax.ppermute(shard, axis, pairs)


def body(train_cores, sketch_cores, left_interface, right_sketch):
    my_core = train_cores[0]
    my_sketch = sketch_cores[0]
    rank_size = my_core.shape[0]
    mode_local = my_core.shape[1]
    sketch_size = my_sketch.shape[0]
    group_index = lax.axis_index("cores")
    group_count = lax.axis_size("cores")
    final_group = group_count - 1
    flat_core = my_core.reshape(rank_size * mode_local, rank_size)
    sketch_flat = my_sketch.reshape(sketch_size, mode_local * sketch_size)
    sketch = right_sketch
    for round_index in range(group_count - 1):
        partial_value = jnp.dot(flat_core, sketch, preferred_element_type=jnp.float32).astype(
            jnp.bfloat16
        )
        partial_value = partial_value.reshape(rank_size, mode_local * sketch_size)
        local_term = lax.dot_general(
            partial_value, sketch_flat, (((1,), (1,)), ((), ())), preferred_element_type=jnp.float32
        )
        summed = lax.psum(local_term, "mode")
        received = from_behind(summed.astype(jnp.bfloat16), "cores", -1)
        sketch = jnp.where(group_index == final_group, right_sketch, received)
    frame_scale = math.sqrt(sketch_size * mode_local * lax.axis_size("mode"))
    wide_core = my_core.reshape(rank_size, mode_local * rank_size)
    interface = left_interface
    for round_index in range(group_count):
        carry_low = interface.astype(jnp.bfloat16)
        built = jnp.dot(carry_low, wide_core, preferred_element_type=jnp.float32)
        built = built.astype(jnp.bfloat16).reshape(sketch_size * mode_local, rank_size)
        images = jnp.dot(built, sketch, preferred_element_type=jnp.float32)
        core_local = lax.dot_general(
            built, built, (((0,), (0,)), ((), ())), preferred_element_type=jnp.float32
        )
        core_square = lax.psum(core_local, "mode")
        sketch_wide = sketch.astype(jnp.float32)
        projected = lax.dot_general(
            sketch_wide, core_square, (((0,), (0,)), ((), ())), precision=lax.Precision.HIGHEST
        )
        gram_matrix = jnp.dot(projected, sketch_wide, precision=lax.Precision.HIGHEST)
        chol_lower = jnp.linalg.cholesky(gram_matrix)
        frame_rows = lax.linalg.triangular_solve(chol_lower, images.T, left_side=True, lower=True)
        next_interface = lax.linalg.triangular_solve(
            chol_lower, projected, left_side=True, lower=True
        )
        frame_out = (frame_rows.T * frame_scale).astype(jnp.bfloat16)
        interface_out = next_interface
        if round_index < group_count - 1:
            passed = from_behind(next_interface.astype(jnp.bfloat16), "cores", 1)
            interface = jnp.where(group_index == 0, left_interface, passed.astype(jnp.float32))
    frames = frame_out.reshape(1, sketch_size, mode_local, sketch_size)
    interfaces = interface_out.reshape(1, sketch_size, rank_size)
    return (frames, interfaces)


def solution(mesh):
    in_specs = (P("cores", None, "mode", None), P("cores", None, "mode", None), P(), P())
    out_specs = (P("cores", None, "mode", None), P("cores", None, None))
    return jax.shard_map(body, mesh=mesh, in_specs=in_specs, out_specs=out_specs, check_vma=False)
```

profile of v0, /device:TPU:0, one launch (start us, length us, event | category | flops | bytes accessed | tf_op | source)
XLA Modules:
  0.0 529.6 jit_solution(15847679337264826134)
XLA Ops:
  7.2 2.8 reshape_squeeze.9
  11.7 42.0 %all-reduce.15 = bf16[400,100]{1,0:T(8,128)(2,1)} all-reduce(f32[400,100]{1,0:T(8,128)S(1)} %fusion.30), channel_id=1, replica_groups=mesh['mode'=8,'cores'=4] {'mode'}, use_global_device_ids=true, to_apply=%region_0.0 | all-reduce | flops 40000 | bytes 240000 | tf_op jit(solution)/shard_map/psum | solution.py:34
  55.1 3.4 reshape_squeeze.11
  61.2 2.3 fusion
  65.4 2.1 reshape.43
  67.5 2.0 fusion.31
  69.4 36.3 %all-reduce.16 = bf16[400,100]{1,0:T(8,128)(2,1)} all-reduce(f32[400,100]{1,0:T(8,128)} %fusion.31), channel_id=1, replica_groups=mesh['mode'=8,'cores'=4] {'mode'}, use_global_device_ids=true, to_apply=%region_1.2 | all-reduce | flops 40000 | bytes 240000 | tf_op jit(solution)/shard_map/psum | solution.py:34
  112.0 40.1 %all-reduce.17 = bf16[400,100]{1,0:T(8,128)(2,1)S(1)} all-reduce(f32[400,100]{1,0:T(8,128)S(1)} %fusion.32), channel_id=1, replica_groups=mesh['mode'=8,'cores'=4] {'mode'}, use_global_device_ids=true, to_apply=%region_2.3 | all-reduce | flops 40000 | bytes 240000 | tf_op jit(solution)/shard_map/psum | solution.py:34
  155.4 31.4 %all-reduce.8.cloned.1.call-done = f32[400,400]{1,0:T(8,128)} async-done(((f32[400,400]{1,0:T(8,128)}), f32[400,400]{1,0:T(8,128)}) %all-reduce.8.cloned.1.call-update) | async-done | bytes 640016 | tf_op jit(solution)/shard_map/psum | solution.py:48
  186.9 2.1 fusion.34
  189.5 9.1 %cholesky.74 = f32[100,100]{1,0:T(8,128)S(1)} custom-call(f32[100,100]{1,0:T(8,128)S(1)} %fusion.23), custom_call_target="Cholesky" | custom-call | tf_op jit(solution)/shard_map/jit(cholesky)/cholesky | solution.py:54
  200.0 7.7 %custom-call.9 = f32[1,100,100]{1,2,0:T(8,128)S(1)} custom-call(f32[1,100,100]{2,1,0:T(8,128)S(1)} %fusion.11), custom_call_target="InvertDiagBlocksLowerTriangular" | custom-call | tf_op jit(solution)/shard_map/triangular_solve/custom-call.0 | solution.py:56
  212.5 78.7 %all-reduce.10.cloned.1.call-done = f32[400,400]{1,0:T(8,128)} async-done(((f32[400,400]{1,0:T(8,128)}), f32[400,400]{1,0:T(8,128)}) %all-reduce.10.cloned.1.call-update) | async-done | bytes 640016 | tf_op jit(solution)/shard_map/psum | solution.py:48
  291.2 2.1 fusion.37
  293.9 9.1 %cholesky.85 = f32[100,100]{1,0:T(8,128)S(1)} custom-call(f32[100,100]{1,0:T(8,128)S(1)} %fusion.21), custom_call_target="Cholesky" | custom-call | tf_op jit(solution)/shard_map/jit(cholesky)/cholesky | solution.py:54
  304.4 7.7 %custom-call.10 = f32[1,100,100]{1,2,0:T(8,128)S(1)} custom-call(f32[1,100,100]{2,1,0:T(8,128)S(1)} %fusion.12), custom_call_target="InvertDiagBlocksLowerTriangular" | custom-call | tf_op jit(solution)/shard_map/triangular_solve/custom-call.0 | solution.py:56
  317.1 78.5 %all-reduce.12.cloned.1.call-done = f32[400,400]{1,0:T(8,128)} async-done(((f32[400,400]{1,0:T(8,128)}), f32[400,400]{1,0:T(8,128)}) %all-reduce.12.cloned.1.call-update) | async-done | bytes 640016 | tf_op jit(solution)/shard_map/psum | solution.py:48
  395.6 2.1 fusion.40
  398.2 9.1 %cholesky.96 = f32[100,100]{1,0:T(8,128)S(1)} custom-call(f32[100,100]{1,0:T(8,128)S(1)} %fusion.19), custom_call_target="Cholesky" | custom-call | tf_op jit(solution)/shard_map/jit(cholesky)/cholesky | solution.py:54
  408.7 7.7 %custom-call.11 = f32[1,100,100]{1,2,0:T(8,128)S(1)} custom-call(f32[1,100,100]{2,1,0:T(8,128)S(1)} %fusion.13), custom_call_target="InvertDiagBlocksLowerTriangular" | custom-call | tf_op jit(solution)/shard_map/triangular_solve/custom-call.0 | solution.py:56
  421.5 78.5 %all-reduce.14.cloned.1.call-done = f32[400,400]{1,0:T(8,128)} async-done(((f32[400,400]{1,0:T(8,128)}), f32[400,400]{1,0:T(8,128)}) %all-reduce.14.cloned.1.call-update) | async-done | bytes 640016 | tf_op jit(solution)/shard_map/psum | solution.py:48
  499.9 2.1 fusion.43
  502.6 9.1 %cholesky.107 = f32[100,100]{1,0:T(8,128)S(1)} custom-call(f32[100,100]{1,0:T(8,128)S(1)} %fusion.17), custom_call_target="Cholesky" | custom-call | tf_op jit(solution)/shard_map/jit(cholesky)/cholesky | solution.py:54
  513.0 7.7 %custom-call.12 = f32[1,100,100]{1,2,0:T(8,128)S(1)} custom-call(f32[1,100,100]{2,1,0:T(8,128)S(1)} %fusion.14), custom_call_target="InvertDiagBlocksLowerTriangular" | custom-call | tf_op jit(solution)/shard_map/triangular_solve/custom-call.0 | solution.py:55
  (88 shorter events, 41.7 us)
Async XLA Ops:
  7.2 2.9 copy-start.4
  7.2 179.7 %all-reduce.8.cloned.1.call-start = ((), (), s32[]{:S(2)}) async-start(), calls=%async_computation | async-start | bytes 1638400 | tf_op jit(solution)/shard_map/psum | solution.py:48
  10.1 1.2 copy-start.6
  11.4 42.3 %copy-start.2 = (bf16[100,400]{1,0:T(8,128)(2,1)}, bf16[100,400]{1,0:T(8,128)(2,1)S(1)}, u32[]{:S(2)}) copy-start(bf16[100,400]{1,0:T(8,128)(2,1)S(1)} %reshape.69) | copy-start | bytes 240004
  53.7 4.8 copy-start
  53.7 7.5 %collective-permute-start = (bf16[400,100]{1,0:T(8,128)(2,1)}, bf16[400,100]{1,0:T(8,128)(2,1)}, u32[]{:S(2)}, u32[]{:S(2)}) collective-permute-start(bf16[400,100]{1,0:T(8,128)(2,1)} %all-reduce.15), channel_id=1, source_target_pairs={{1,0},{2,1},{3,2},{5,4},{6,5},{7,6},{9,8},{10,9},{11,10},{13,12},{... | collective-permute-start | bytes 240008 | tf_op jit(solution)/shard_map/ppermute | solution.py:11
  105.7 3.5 collective-permute-start.1
  108.4 182.9 %all-reduce.10.cloned.1.call-start = ((), (), s32[]{:S(2)}) async-start(), calls=%async_computation.1 | async-start | bytes 1638400 | tf_op jit(solution)/shard_map/psum | solution.py:48
  110.8 0.9 copy-start.3
  110.8 44.6 %copy-start.5 = (bf16[400,100]{1,0:T(8,128)(2,1)S(1)}, bf16[400,100]{1,0:T(8,128)(2,1)}, u32[]{:S(2)}) copy-start(bf16[400,100]{1,0:T(8,128)(2,1)} %param.10) | copy-start | bytes 240004
  152.1 58.2 %copy-start.1 = (f32[100,400]{0,1:T(8,128)S(1)}, f32[100,400]{0,1:T(8,128)}, u32[]{:S(2)}) copy-start(f32[100,400]{0,1:T(8,128)} %param.9) | copy-start | bytes 480004
  152.1 3.3 collective-permute-start.2
  208.0 2.2 collective-permute-start.3
  212.5 183.1 %all-reduce.12.cloned.1.call-start = ((), (), s32[]{:S(2)}) async-start(), calls=%async_computation.2 | async-start | bytes 1638400 | tf_op jit(solution)/shard_map/psum | solution.py:48
  312.4 2.5 collective-permute-start.4
  317.1 182.9 %all-reduce.14.cloned.1.call-start = ((), (), s32[]{:S(2)}) async-start(), calls=%async_computation.3 | async-start | bytes 1638400 | tf_op jit(solution)/shard_map/psum | solution.py:48
  416.7 2.2 collective-permute-start.5
Sparse Core Ops, SparseCore 0:
  108.5 78.3 all-reduce.7
  212.6 78.5 all-reduce.9
  317.2 78.3 all-reduce.11
  421.3 78.5 all-reduce.13
where the time goes:
time: 531 us; the launch traced here: 530 us
  waiting for transfers between devices  272 us (51%)
  blocking collectives  118 us (22%)
  other arithmetic  72.6 us (14%)
  matrix products  27.2 us (5%)
  local copies, waits for them, and re-layouts  16 us (3%)
  between operations  14.3 us (3%)
  starting transfers between devices  8.83 us (2%)
    psum x4, waiting for transfers between devices, body(): core_square = lax.psum(core_local, 'mode')  267 us
    psum x3, blocking collectives, body(): summed = lax.psum(local_term, 'mode')  118 us
    another operation x12, other arithmetic, body(): chol_lower = jnp.linalg.cholesky(gram_matrix)  39.3 us
    another operation x6, other arithmetic, body(): lax.linalg.triangular_solve(chol_lower, projected, left_side=True, lower=...  25 us
  transfers between devices with their start and end apart: 10, of which 9 were waited for; matrix products, arithmetic and copies ran while one was open for 2% of the time, Pallas kernels for 0%

commit v1 on v0

--- a/solution.py
+++ b/solution.py
@@ -31,7 +31,7 @@
         local_term = lax.dot_general(
             partial_value, sketch_flat, (((1,), (1,)), ((), ())), preferred_element_type=jnp.float32
         )
-        summed = lax.psum(local_term, "mode")
+        summed = jnp.sum(lax.all_gather(local_term, "mode"), axis=0)
         received = from_behind(summed.astype(jnp.bfloat16), "cores", -1)
         sketch = jnp.where(group_index == final_group, right_sketch, received)
     frame_scale = math.sqrt(sketch_size * mode_local * lax.axis_size("mode"))

time: 531 us -> 584 us (1.100)
  waiting for transfers between devices: 272 us -> 450 us
  blocking collectives: 118 us -> 0 us
  local copies, waits for them, and re-layouts: 16 us -> 9.42 us
    all_gather x0 -> x3, waiting for transfers between devices: none -> 133 us  [body(): summed = jnp.sum(lax.all_gather(local_term, 'mode'), axis=0)]
    psum x3 -> x0, blocking collectives: 118 us -> none  [body(): summed = lax.psum(local_term, 'mode')]
    psum x4, waiting for transfers between devices: 267 us -> 308 us  [body(): core_square = lax.psum(core_local, 'mode')]
  transfers between devices with their start and end apart: 10 -> 13, of which waited for: 9 -> 13; matrix products, arithmetic and copies ran while one was open for 2% -> 1% of each run, Pallas kernels for 0% -> 0%
where the time goes in v1:
time: 584 us
  waiting for transfers between devices  450 us (77%)
  other arithmetic  77.3 us (13%)
  matrix products  24.4 us (4%)
  between operations  14.6 us (2%)
  local copies, waits for them, and re-layouts  9.42 us (2%)
  starting transfers between devices  8.45 us (1%)
    psum x4, waiting for transfers between devices, body(): core_square = lax.psum(core_local, 'mode')  308 us
    all_gather x3, waiting for transfers between devices, body(): summed = jnp.sum(lax.all_gather(local_term, 'mode'), axis=0)  133 us
    another operation x12, other arithmetic, body(): chol_lower = jnp.linalg.cholesky(gram_matrix)  39.3 us
    another operation x6, other arithmetic, body(): lax.linalg.triangular_solve(chol_lower, projected, left_side=True, lower=...  25 us
  transfers between devices with their start and end apart: 13, of which 13 were waited for; matrix products, arithmetic and copies ran while one was open for 1% of the time, Pallas kernels for 0%

profile of v1, /device:TPU:0, one launch (start us, length us, event | category | flops | bytes accessed | tf_op | source)
XLA Modules:
  0.0 583.8 jit_solution(4911555481705809838)
XLA Ops:
  7.2 2.8 reshape_squeeze.9
  12.4 47.7 %all-gather.7.cloned.1.call-done = f32[3200,100]{1,0:T(8,128)} async-done(((f32[400,100]{1,0:T(8,128)}), f32[3200,100]{1,0:T(8,128)}) %all-gather.7.cloned.1.call-update) | async-done | bytes 1280016 | tf_op jit(solution)/shard_map/all_gather | solution.py:34
  62.9 1.9 collective-permute-done
  67.1 44.7 %all-gather.9.cloned.1.call-done = f32[3200,100]{1,0:T(8,128)} async-done(((f32[400,100]{1,0:T(8,128)}), f32[3200,100]{1,0:T(8,128)}) %all-gather.9.cloned.1.call-update) | async-done | bytes 1280016 | tf_op jit(solution)/shard_map/all_gather | solution.py:34
  114.6 1.9 collective-permute-done.1
  118.8 1.6 reshape_squeeze.11
  122.7 40.8 %all-gather.11.cloned.1.call-done = f32[3200,100]{1,0:T(8,128)} async-done(((f32[400,100]{1,0:T(8,128)}), f32[3200,100]{1,0:T(8,128)}) %all-gather.11.cloned.1.call-update) | async-done | bytes 1280016 | tf_op jit(solution)/shard_map/all_gather | solution.py:34
  166.3 1.9 collective-permute-done.2
  168.2 72.5 %all-reduce.5.cloned.1.call-done = f32[400,400]{1,0:T(8,128)} async-done(((f32[400,400]{1,0:T(8,128)}), f32[400,400]{1,0:T(8,128)}) %all-reduce.5.cloned.1.call-update) | async-done | bytes 640016 | tf_op jit(solution)/shard_map/psum | solution.py:48
  240.7 2.1 fusion.34
  243.3 9.1 %cholesky.74 = f32[100,100]{1,0:T(8,128)S(1)} custom-call(f32[100,100]{1,0:T(8,128)S(1)} %fusion.23), custom_call_target="Cholesky" | custom-call | tf_op jit(solution)/shard_map/jit(cholesky)/cholesky | solution.py:54
  253.8 7.7 %custom-call.9 = f32[1,100,100]{1,2,0:T(8,128)S(1)} custom-call(f32[1,100,100]{2,1,0:T(8,128)S(1)} %fusion.11), custom_call_target="InvertDiagBlocksLowerTriangular" | custom-call | tf_op jit(solution)/shard_map/triangular_solve/custom-call.0 | solution.py:56
  266.4 78.7 %all-reduce.7.cloned.1.call-done = f32[400,400]{1,0:T(8,128)} async-done(((f32[400,400]{1,0:T(8,128)}), f32[400,400]{1,0:T(8,128)}) %all-reduce.7.cloned.1.call-update) | async-done | bytes 640016 | tf_op jit(solution)/shard_map/psum | solution.py:48
  345.1 2.1 fusion.37
  347.7 9.1 %cholesky.85 = f32[100,100]{1,0:T(8,128)S(1)} custom-call(f32[100,100]{1,0:T(8,128)S(1)} %fusion.21), custom_call_target="Cholesky" | custom-call | tf_op jit(solution)/shard_map/jit(cholesky)/cholesky | solution.py:54
  358.2 7.7 %custom-call.10 = f32[1,100,100]{1,2,0:T(8,128)S(1)} custom-call(f32[1,100,100]{2,1,0:T(8,128)S(1)} %fusion.12), custom_call_target="InvertDiagBlocksLowerTriangular" | custom-call | tf_op jit(solution)/shard_map/triangular_solve/custom-call.0 | solution.py:56
  370.7 78.7 %all-reduce.9.cloned.1.call-done = f32[400,400]{1,0:T(8,128)} async-done(((f32[400,400]{1,0:T(8,128)}), f32[400,400]{1,0:T(8,128)}) %all-reduce.9.cloned.1.call-update) | async-done | bytes 640016 | tf_op jit(solution)/shard_map/psum | solution.py:48
  449.4 2.1 fusion.40
  452.0 9.1 %cholesky.96 = f32[100,100]{1,0:T(8,128)S(1)} custom-call(f32[100,100]{1,0:T(8,128)S(1)} %fusion.19), custom_call_target="Cholesky" | custom-call | tf_op jit(solution)/shard_map/jit(cholesky)/cholesky | solution.py:54
  462.5 7.7 %custom-call.11 = f32[1,100,100]{1,2,0:T(8,128)S(1)} custom-call(f32[1,100,100]{2,1,0:T(8,128)S(1)} %fusion.13), custom_call_target="InvertDiagBlocksLowerTriangular" | custom-call | tf_op jit(solution)/shard_map/triangular_solve/custom-call.0 | solution.py:56
  475.3 78.5 %all-reduce.11.cloned.1.call-done = f32[400,400]{1,0:T(8,128)} async-done(((f32[400,400]{1,0:T(8,128)}), f32[400,400]{1,0:T(8,128)}) %all-reduce.11.cloned.1.call-update) | async-done | bytes 640016 | tf_op jit(solution)/shard_map/psum | solution.py:48
  553.8 2.1 fusion.43
  556.4 9.1 %cholesky.107 = f32[100,100]{1,0:T(8,128)S(1)} custom-call(f32[100,100]{1,0:T(8,128)S(1)} %fusion.17), custom_call_target="Cholesky" | custom-call | tf_op jit(solution)/shard_map/jit(cholesky)/cholesky | solution.py:54
  566.9 7.7 %custom-call.12 = f32[1,100,100]{1,2,0:T(8,128)S(1)} custom-call(f32[1,100,100]{2,1,0:T(8,128)S(1)} %fusion.14), custom_call_target="InvertDiagBlocksLowerTriangular" | custom-call | tf_op jit(solution)/shard_map/triangular_solve/custom-call.0 | solution.py:55
  (91 shorter events, 41.9 us)
Async XLA Ops:
  7.2 2.9 copy-start.2
  7.2 52.9 %all-gather.7.cloned.1.call-start = ((), (), s32[]{:S(2)}) async-start(), calls=%async_computation.4 | async-start | bytes 1843200 | tf_op jit(solution)/shard_map/all_gather | solution.py:34
  10.1 1.2 copy-start.3
  12.4 99.4 %all-gather.9.cloned.1.call-start = ((), (), s32[]{:S(2)}) async-start(), calls=%async_computation.5 | async-start | bytes 1843200 | tf_op jit(solution)/shard_map/all_gather | solution.py:34
  61.6 3.2 collective-permute-start
  67.0 96.4 %all-gather.11.cloned.1.call-start = ((), (), s32[]{:S(2)}) async-start(), calls=%async_computation.6 | async-start | bytes 1843200 | tf_op jit(solution)/shard_map/all_gather | solution.py:34
  113.3 3.2 collective-permute-start.1
  117.2 1.6 copy-start
  118.7 1.7 copy-start.1
  118.7 122.0 %all-reduce.5.cloned.1.call-start = ((), (), s32[]{:S(2)}) async-start(), calls=%async_computation | async-start | bytes 1638400 | tf_op jit(solution)/shard_map/psum | solution.py:48
  122.6 222.4 %all-reduce.7.cloned.1.call-start = ((), (), s32[]{:S(2)}) async-start(), calls=%async_computation.1 | async-start | bytes 1638400 | tf_op jit(solution)/shard_map/psum | solution.py:48
  165.0 3.2 collective-permute-start.2
  261.8 2.2 collective-permute-start.3
  266.3 183.1 %all-reduce.9.cloned.1.call-start = ((), (), s32[]{:S(2)}) async-start(), calls=%async_computation.2 | async-start | bytes 1638400 | tf_op jit(solution)/shard_map/psum | solution.py:48
  366.2 2.2 collective-permute-start.4
  370.7 183.1 %all-reduce.11.cloned.1.call-start = ((), (), s32[]{:S(2)}) async-start(), calls=%async_computation.3 | async-start | bytes 1638400 | tf_op jit(solution)/shard_map/psum | solution.py:48
  470.5 2.2 collective-permute-start.5
Sparse Core Ops, SparseCore 0:
  12.5 47.5 all-gather.6
  67.1 44.5 all-gather.8
  118.8 44.5 all-gather.10
  166.8 73.8 all-reduce.4
  266.4 78.5 all-reduce.6
  370.8 78.5 all-reduce.8
  475.1 78.6 all-reduce.10
